TPU v7x, 32 devices: a whole 2x2x4 slice. The times are simulated.
32 devices in a mesh: groups: 2 (over y), seq: 4 (over z), head: 4 (over x, core).
Axes of the slice: x: 2, y: 2, z: 4, core: 2. Of those that a mesh axis runs over, the one named last changes fastest.
Arguments:
- queries: bfloat16 [2048, 8192], P(('groups', 'seq'), 'head'), parts along dimension 0, may hold values from -16 to 16
- keys: bfloat16 [2048, 1024], P(('groups', 'seq'), 'head'), parts along dimension 0, may hold values from -16 to 16
- values: bfloat16 [2048, 1024], P(('groups', 'seq'), 'head'), parts along dimension 0, may hold values from -6 to 6
- prompt_len: int32 [2], P('groups'), parts along dimension 0, may hold values from 256 to 1024
- page_dest: int32 [8, 2], P('groups'), parts along dimension 0, may hold values from 0 to 3, all different within a row; in each aligned block of 4 rows (0 to 3, 4 to 7, ...) at most 4 rows name the same one
Outputs:
- attended: bfloat16 [2048, 8192], P(('groups', 'seq'), 'head'), parts along dimension 0
- decode_page_cache: bfloat16 [32, 128, 2048], P(('groups', 'seq'), None, 'head'), parts along dimension 0
There are 2 independent parts, one for each index of `groups`. A program takes and returns all parts, laid end to end along the dimension named above; each array names one. Nothing has to cross between parts.
Inputs may be any that keep to these rules, and one draw needn't show every extreme that they name: `page_dest`: row s names the decode devices of the 2 pages of tokens s * 256 to (s + 1) * 256 - 1, all different within a row; no device is named more than 4 times in all, and some device exactly 4 times.
All inputs are finite; a program needn't handle non-finite values.
Results may differ from a plain program's by a relative error of at most 0.005.
Values may be sent and summed in bfloat16 or wider, within the bound.
A program may use at most 64 MiB of HBM per device.

v0:
```python
import math
import jax
import jax.numpy as jnp
from jax import lax
from jax.sharding import PartitionSpec as P

HEAD_SIZE = 128
PAGE_TOKENS = 128
NEG_FILL = -1e30


def blank_state(kv_heads, group_size, query_count):
    return (
        jnp.full((kv_heads, group_size, query_count), NEG_FILL, jnp.float32),
        jnp.zeros((kv_heads, group_size, query_count), jnp.float32),
        jnp.zeros((kv_heads, group_size, query_count, HEAD_SIZE), jnp.float32),
    )


def attend_block(
    query_state, query_block, query_pos, key_block, value_block, block_start, prompt_end
):
    key_count = key_block.shape[0]
    kv_heads = key_block.shape[1] // HEAD_SIZE
    keys_split = key_block.reshape(key_count, kv_heads, HEAD_SIZE)
    values_split = value_block.reshape(key_count, kv_heads, HEAD_SIZE)
    scores = jnp.einsum(
        "rkgd,pkd->kgrp", query_block, keys_split, preferred_element_type=jnp.float32
    )
    scores = scores * (1.0 / math.sqrt(HEAD_SIZE))
    key_pos = block_start + jnp.arange(key_count, dtype=jnp.int32)
    allowed = (key_pos[None, :] <= query_pos[:, None]) & (key_pos[None, :] < prompt_end)
    scores = jnp.where(allowed, scores, NEG_FILL)
    old_max = query_state[0]
    new_max = jnp.maximum(old_max, jnp.max(scores, axis=-1))
    weights = jnp.where(allowed, jnp.exp(scores - new_max[..., None]), 0.0)
    factor = jnp.exp(old_max - new_max)
    denominator = query_state[1] * factor + jnp.sum(weights, axis=-1)
    accumulated = query_state[2] * factor[..., None] + jnp.einsum(
        "kgrp,pkd->kgrd",
        weights.astype(jnp.bfloat16),
        values_split,
        preferred_element_type=jnp.float32,
    )
    return (new_max, denominator, accumulated)


def finish(query_state, query_pos, prompt_end):
    query_live = query_pos < prompt_end
    safe_total = jnp.where(query_live[None, None, :], query_state[1], 1.0)
    result = jnp.where(query_live[None, None, :, None], query_state[2] / safe_total[..., None], 0.0)
    query_count = query_pos.shape[0]
    return result.transpose(2, 0, 1, 3).reshape(query_count, -1).astype(jnp.bfloat16)


def join_pages(key_rows, value_rows):
    page_count = key_rows.shape[0] // PAGE_TOKENS
    kv_heads = key_rows.shape[1] // HEAD_SIZE
    stacked = jnp.stack(
        (
            key_rows.reshape(page_count, PAGE_TOKENS, kv_heads, HEAD_SIZE),
            value_rows.reshape(page_count, PAGE_TOKENS, kv_heads, HEAD_SIZE),
        ),
        axis=3,
    )
    return stacked.reshape(page_count, PAGE_TOKENS, 2 * key_rows.shape[1])


def slot_pages(page_dest, owner, slots):
    flat_dest = page_dest.reshape(-1)
    page_order = jnp.arange(flat_dest.shape[0], dtype=jnp.int32)
    same_dest = flat_dest[:, None] == flat_dest[None, :]
    dest_rank = jnp.sum(same_dest & (page_order[None, :] < page_order[:, None]), axis=1)
    matched = (flat_dest[:, None] == owner) & (
        dest_rank[:, None] == jnp.arange(slots, dtype=jnp.int32)[None, :]
    )
    page_index = jnp.sum(jnp.where(matched, page_order[:, None], 0), axis=0)
    present = jnp.any(matched, axis=0)
    return (flat_dest, page_index, present)


def place_pages(stored, key_block, value_block, block_start, prompt_end, page_index, present):
    key_pos = block_start + jnp.arange(key_block.shape[0], dtype=jnp.int32)
    token_present = (key_pos < prompt_end)[:, None]
    block_pages = join_pages(
        jnp.where(token_present, key_block, 0), jnp.where(token_present, value_block, 0)
    )
    page_count = block_pages.shape[0]
    local_index = page_index - block_start // PAGE_TOKENS
    inside = present & (local_index >= 0) & (local_index < page_count)
    picked = block_pages[jnp.clip(local_index, 0, page_count - 1)]
    return jnp.where(inside[:, None, None], picked, stored)


def local(queries, keys, values, prompt_len, page_dest):
    shard_rows = queries.shape[0]
    kv_width = keys.shape[1]
    kv_heads = kv_width // HEAD_SIZE
    group_size = queries.shape[1] // kv_width
    seq_index = lax.axis_index("seq")
    prompt_end = prompt_len[0]
    per_device = page_dest.shape[1]
    slots = 2 * per_device
    flat_dest, page_index, present = slot_pages(page_dest, seq_index, slots)
    own_rows = seq_index * shard_rows + jnp.arange(shard_rows, dtype=jnp.int32)
    query_parts = (queries,)
    positions = (own_rows,)
    shaped = tuple(
        (
            part_rows.reshape(part_rows.shape[0], kv_heads, group_size, HEAD_SIZE)
            for part_rows in query_parts
        )
    )
    states = tuple(
        (blank_state(kv_heads, group_size, part_rows.shape[0]) for part_rows in query_parts)
    )
    page_store = jnp.zeros((slots, PAGE_TOKENS, 2 * kv_width), jnp.bfloat16)
    key_piece = lax.all_gather(keys, "seq", axis=0, tiled=True)
    value_piece = lax.all_gather(values, "seq", axis=0, tiled=True)
    block_count = key_piece.shape[0] // shard_rows
    per_step = max(1, min(block_count, 512 // shard_rows))
    while block_count % per_step:
        per_step -= 1
    step_rows = per_step * shard_rows
    steps_count = block_count // per_step
    key_blocks = key_piece.reshape(steps_count, step_rows, kv_width)
    value_blocks = value_piece.reshape(steps_count, step_rows, kv_width)

    def one_block(inner_carry, block_item):
        block_states, stored = inner_carry
        key_block, value_block, number = block_item
        block_start = number * step_rows
        updated = []
        for query_state, query_block, query_pos in zip(block_states, shaped, positions):
            needed = block_start <= jnp.minimum(query_pos[-1], prompt_end - 1)
            updated.append(
                lax.cond(
                    needed,
                    lambda kept: attend_block(
                        kept,
                        query_block,
                        query_pos,
                        key_block,
                        value_block,
                        block_start,
                        prompt_end,
                    ),
                    lambda kept: kept,
                    query_state,
                )
            )
        stored = place_pages(
            stored, key_block, value_block, block_start, prompt_end, page_index, present
        )
        return ((tuple(updated), stored), None)

    result, unused = lax.scan(
        one_block,
        (states, page_store),
        (key_blocks, value_blocks, jnp.arange(steps_count, dtype=jnp.int32)),
    )
    final_states, stored = result
    outputs = [
        finish(query_state, query_pos, prompt_end)
        for query_state, query_pos in zip(final_states, positions)
    ]
    attended = outputs[0]
    return (attended, stored)


def solution(mesh):
    return jax.shard_map(
        local,
        mesh=mesh,
        in_specs=(
            P(("groups", "seq"), "head"),
            P(("groups", "seq"), "head"),
            P(("groups", "seq"), "head"),
            P("groups"),
            P("groups", None),
        ),
        out_specs=(P(("groups", "seq"), "head"), P(("groups", "seq"), None, "head")),
        check_vma=False,
    )
```

profile of v0, /device:TPU:26, one launch (start us, length us, event | category | flops | bytes accessed | tf_op | source)
XLA Modules:
  0.0 76.9 jit_solution(3035175965505265752)
XLA Ops:
  1.3 0.7 slice.5
  2.7 0.8 copy.34
  3.4 0.1 broadcast_in_dim_reshape.2
  3.5 0.2 convert_reduce_fusion
  3.7 0.1 fusion.20
  3.8 0.1 select_reduce_fusion
  4.0 16.3 %all_gather.6 = bf16[1024,256]{1,0:T(8,128)(2,1)} all-gather(bf16[256,256]{1,0:T(8,128)(2,1)} %param.10), channel_id=1, replica_groups=mesh['groups'=2,'seq'=4,'head'=4] {'seq'}, dimensions={0}, use_global_device_ids=true | all-gather | bytes 655360 | tf_op jit(solution)/shard_map/all_gather | solution.py:118
  20.3 16.4 %all_gather.7 = bf16[1024,256]{1,0:T(8,128)(2,1)} all-gather(bf16[256,256]{1,0:T(8,128)(2,1)} %param.11), channel_id=1, replica_groups=mesh['groups'=2,'seq'=4,'head'=4] {'seq'}, dimensions={0}, use_global_device_ids=true | all-gather | bytes 655360 | tf_op jit(solution)/shard_map/all_gather | solution.py:119
  36.7 1.5 %copy.33 = bf16[256,2048]{0,1:T(8,128)(2,1)S(1)} copy(bf16[256,2048]{1,0:T(8,128)(2,1)} %param.9) | data formatting | bytes 2097152 | tf_op args[0]
  38.2 0.7 copy.35
  38.9 1.6 %broadcast_in_dim.106 = f32[2,8,256,128]{3,2,1,0:T(8,128)} broadcast(f32[]{:T(128)} %constant.102.clone.1), dimensions={} | broadcast | bytes 2097156 | tf_op jit(solution)/shard_map/broadcast_in_dim | solution.py:16
  40.4 31.5 %while.20 = (s32[]{:T(128)}, f32[2,8,256]{2,1,0:T(8,128)S(1)}, f32[2,8,256]{2,1,0:T(8,128)S(1)}, f32[2,8,256,128]{3,2,1,0:T(8,128)}, bf16[4,128,512]{1,2,0:T(8,1...) while((s32[]{:T(128)}, f32[2,8,256]{2,1,0:T(8,128)S(1)}, ...), condition=%wide.region_8.9_spmd.clone, body=%wide.region_3.8_spmd.clone.sunk | while | flops 1103377152 | bytes 57424572 | solution.py:157
  40.4 0.7 dynamic_slice.31
  41.9 0.7 add_compare_fusion.2
  42.5 1.1 %constant_dynamic-slice_fusion.3 = (bf16[1,512,256]{2,1,0:T(8,128)(2,1)S(1)}, bf16[1,512,256]{2,1,0:T(8,128)(2,1)S(1)}) fusion(bf16[2,512,256]{2,1,0:T(8,128)(2,1)} %get-tuple-element.556, s32[]{:T(128)S(6)} %copy.67, bf16[2,512,256]{2,1,0:T(8,128)(2,1)} %get-tuple-element.555), kind=kLoop, calls=%fused_computation.31.clone.1 | loop fusion | bytes 1048580 | tf_op jit(solution)/shard_map/while/body/jit(dynamic_index_in_dim)/dynamic_slice | solution.py:157
  43.8 1.1 %broadcast_select_fusion.4 = (bf16[4,128,2,1,128]{4,2,1,0,3:T(2,128)(2,1)S(1)}, bf16[4,128,2,1,128]{4,2,1,0,3:T(2,128)(2,1)S(1)}) fusion(bf16[4,128,2,1,128]{4,2,1,0,3:T(2,128)(2,1)S(1)} %squeeze.31, pred[4,128]{1,0:T(4,128)(4,1)S(1)} %add_compare_fusion.2, bf16[4,128,2,1,128]{4,2,1,0,3:T(2,128)(2,1)S(1)} %squeeze.32), kind=kLoop, calls=%fused_computation.25.clone.1 | loop fusion | flops 262144 | bytes 1049088 | tf_op jit(solution)/shard_map/while/body/eval_jaxpr/jit(_where)/select_n | solution.py:86
  44.9 0.7 pad_maximum_fusion.2
  45.6 0.4 copy.55
  46.1 0.6 gather_fusion
  46.7 0.2 select_select_fusion.2
  46.9 9.3 %conditional.3 = ((f32[2,8,256]{2,1,0:T(8,128)S(1)}, f32[2,8,256]{2,1,0:T(8,128)S(1)}, f32[2,8,256,128]{3,2,1,0:T(8,128)})) conditional(s32[]{:T(128)} %convert_element_type.41, (f32[2,8,256]{2,1,0:T(8,128)S(1)}, f32[2,8,256]{2,1,0:T(8,128)S(1)}, f32[2,8,256,128]{3,2,1,0:T(8,128)}) %tuple.62, (s32[]{:T(128)}, s32[]{:T(128)}, s32[]{:T(128)}, ...), branch_computations={%region_4.4_spmd, %region_5.7_spmd} | conditional | flops 1102325504 | bytes 49553512 | solution.py:137
  46.9 0.7 broadcast_compare_fusion
  47.6 0.2 compare_and_fusion
  47.9 0.1 reshape.145
  48.0 1.4 %fusion.2 = (f32[2,8,256]{2,1,0:T(8,128)S(1)}, f32[2,512,256,8]{2,1,3,0:T(8,128)S(1)}) fusion(pred[256,512]{0,1:T(8,128)(4,1)S(1)} %compare_and_fusion, bf16[256,2,8,128]{3,0,2,1:T(8,128)(2,1)S(1)} %get-tuple-element.235, bf16[512,2,128,1]{2,1,0,3:T(2,128)(2,1)S(1)} %bitcast.45), kind=kOutput, calls=%fused_computation.4 | convolution fusion | flops 543158272 | bytes 9846784 | tf_op jit(solution)/shard_map/while/body/eval_jaxpr/cond/branch_1_fun/rkgd,pkd->kgrp/dot_general | solution.py:27
  49.4 2.0 %fusion.4 = f32[2,8,256]{2,1,0:T(8,128)S(1)} fusion(f32[2,512,256,8]{2,1,3,0:T(8,128)S(1)} %get-tuple-element.398, f32[2,8,256]{2,1,0:T(8,128)S(1)} %max.6, pred[256,512]{0,1:T(8,128)(4,1)S(1)} %compare_and_fusion), kind=kLoop, calls=%fused_computation.6 | loop fusion | flops 10481664 | bytes 8552448 | tf_op jit(solution)/shard_map/while/body/eval_jaxpr/cond/branch_1_fun/reduce_sum | solution.py:38
  51.4 3.4 %multiply_add_fusion = f32[2,8,256,128]{3,2,1,0:T(8,128)S(1)} fusion(f32[2,8,256,128]{3,2,1,0:T(8,128)S(1)} %copy-done, f32[2,512,256,8]{2,1,3,0:T(8,128)S(1)} %get-tuple-element.398, f32[2,8,256]{2,1,0:T(8,128)S(1)} %max.6, pred[256,512]{0,1:T(8,128)(4,1)S(1)} %compare_and_fusion, f32[2,8,256]{2,1,0:T(8,128)S(1)} %get-tuple-element.396, ...), kind=kOutput, calls=%fused_computation.9 | convolution fusion | flops 548405248 | bytes 13008896 | tf_op jit(solution)/shard_map/while/body/eval_jaxpr/cond/branch_1_fun/kgrp,pkd->kgrd/dot_general | solution.py:39
  54.9 1.3 %copy-done.1 = f32[2,8,256,128]{3,2,1,0:T(8,128)} copy-done((f32[2,8,256,128]{3,2,1,0:T(8,128)}, f32[2,8,256,128]{3,2,1,0:T(8,128)S(1)}, u32[]{:S(2)}) %copy-start.1) | copy-done | bytes 2097176 | tf_op jit(solution)/shard_map/while/body/eval_jaxpr/cond
  56.2 0.7 dynamic_slice.31
  57.6 0.7 add_compare_fusion.2
  58.3 1.1 %constant_dynamic-slice_fusion.3 = (bf16[1,512,256]{2,1,0:T(8,128)(2,1)S(1)}, bf16[1,512,256]{2,1,0:T(8,128)(2,1)S(1)}) fusion(bf16[2,512,256]{2,1,0:T(8,128)(2,1)} %get-tuple-element.556, s32[]{:T(128)S(6)} %copy.67, bf16[2,512,256]{2,1,0:T(8,128)(2,1)} %get-tuple-element.555), kind=kLoop, calls=%fused_computation.31.clone.1 | loop fusion | bytes 1048580 | tf_op jit(solution)/shard_map/while/body/jit(dynamic_index_in_dim)/dynamic_slice | solution.py:157
  59.5 1.1 %broadcast_select_fusion.4 = (bf16[4,128,2,1,128]{4,2,1,0,3:T(2,128)(2,1)S(1)}, bf16[4,128,2,1,128]{4,2,1,0,3:T(2,128)(2,1)S(1)}) fusion(bf16[4,128,2,1,128]{4,2,1,0,3:T(2,128)(2,1)S(1)} %squeeze.31, pred[4,128]{1,0:T(4,128)(4,1)S(1)} %add_compare_fusion.2, bf16[4,128,2,1,128]{4,2,1,0,3:T(2,128)(2,1)S(1)} %squeeze.32), kind=kLoop, calls=%fused_computation.25.clone.1 | loop fusion | flops 262144 | bytes 1049088 | tf_op jit(solution)/shard_map/while/body/eval_jaxpr/jit(_where)/select_n | solution.py:86
  60.6 0.7 pad_maximum_fusion.2
  61.4 0.4 copy.55
  61.8 0.6 gather_fusion
  62.5 0.2 select_select_fusion.2
  62.7 9.3 %conditional.3 = ((f32[2,8,256]{2,1,0:T(8,128)S(1)}, f32[2,8,256]{2,1,0:T(8,128)S(1)}, f32[2,8,256,128]{3,2,1,0:T(8,128)})) conditional(s32[]{:T(128)} %convert_element_type.41, (f32[2,8,256]{2,1,0:T(8,128)S(1)}, f32[2,8,256]{2,1,0:T(8,128)S(1)}, f32[2,8,256,128]{3,2,1,0:T(8,128)}) %tuple.62, (s32[]{:T(128)}, s32[]{:T(128)}, s32[]{:T(128)}, ...), branch_computations={%region_4.4_spmd, %region_5.7_spmd} | conditional | flops 1102325504 | bytes 49553512 | solution.py:137
  62.7 0.7 broadcast_compare_fusion
  63.4 0.2 compare_and_fusion
  63.6 0.1 reshape.145
  63.7 1.4 %fusion.2 = (f32[2,8,256]{2,1,0:T(8,128)S(1)}, f32[2,512,256,8]{2,1,3,0:T(8,128)S(1)}) fusion(pred[256,512]{0,1:T(8,128)(4,1)S(1)} %compare_and_fusion, bf16[256,2,8,128]{3,0,2,1:T(8,128)(2,1)S(1)} %get-tuple-element.235, bf16[512,2,128,1]{2,1,0,3:T(2,128)(2,1)S(1)} %bitcast.45), kind=kOutput, calls=%fused_computation.4 | convolution fusion | flops 543158272 | bytes 9846784 | tf_op jit(solution)/shard_map/while/body/eval_jaxpr/cond/branch_1_fun/rkgd,pkd->kgrp/dot_general | solution.py:27
  65.2 2.0 %fusion.4 = f32[2,8,256]{2,1,0:T(8,128)S(1)} fusion(f32[2,512,256,8]{2,1,3,0:T(8,128)S(1)} %get-tuple-element.398, f32[2,8,256]{2,1,0:T(8,128)S(1)} %max.6, pred[256,512]{0,1:T(8,128)(4,1)S(1)} %compare_and_fusion), kind=kLoop, calls=%fused_computation.6 | loop fusion | flops 10481664 | bytes 8552448 | tf_op jit(solution)/shard_map/while/body/eval_jaxpr/cond/branch_1_fun/reduce_sum | solution.py:38
  67.2 3.4 %multiply_add_fusion = f32[2,8,256,128]{3,2,1,0:T(8,128)S(1)} fusion(f32[2,8,256,128]{3,2,1,0:T(8,128)S(1)} %copy-done, f32[2,512,256,8]{2,1,3,0:T(8,128)S(1)} %get-tuple-element.398, f32[2,8,256]{2,1,0:T(8,128)S(1)} %max.6, pred[256,512]{0,1:T(8,128)(4,1)S(1)} %compare_and_fusion, f32[2,8,256]{2,1,0:T(8,128)S(1)} %get-tuple-element.396, ...), kind=kOutput, calls=%fused_computation.9 | convolution fusion | flops 548405248 | bytes 13008896 | tf_op jit(solution)/shard_map/while/body/eval_jaxpr/cond/branch_1_fun/kgrp,pkd->kgrd/dot_general | solution.py:39
  70.6 1.3 %copy-done.1 = f32[2,8,256,128]{3,2,1,0:T(8,128)} copy-done((f32[2,8,256,128]{3,2,1,0:T(8,128)}, f32[2,8,256,128]{3,2,1,0:T(8,128)S(1)}, u32[]{:S(2)}) %copy-start.1) | copy-done | bytes 2097176 | tf_op jit(solution)/shard_map/while/body/eval_jaxpr/cond
  72.0 2.0 %fusion.17 = bf16[256,2,8,128]{3,0,2,1:T(8,128)(2,1)S(1)} fusion(f32[2,8,256,128]{3,2,1,0:T(8,128)} %get-tuple-element.262, f32[2,8,256]{2,1,0:T(8,128)S(1)} %broadcast_select_fusion.2, pred[256]{0:T(512)(128)(4,1)S(1)} %broadcast_compare_fusion.1), kind=kLoop, calls=%fused_computation.35 | loop fusion | flops 1572864 | bytes 3162368 | tf_op jit(solution)/shard_map/convert_element_type | solution.py:53
  74.0 0.7 copy.36
  74.7 1.2 %copy.53 = bf16[32,8,16,128]{3,1,2,0:T(8,128)(2,1)} copy(bf16[32,8,16,128]{3,2,1,0:T(8,128)(2,1)S(1)} %bitcast.47) | data formatting | bytes 2097152
  75.9 1.0 %copy.37 = bf16[4,128,512]{2,1,0:T(8,128)(2,1)} copy(bf16[4,128,512]{1,2,0:T(8,128)(2,1)S(1)} %get-tuple-element.363) | data formatting | bytes 1048576
  (38 shorter events, 0.6 us)
Async XLA Ops:
  47.9 3.5 %copy-start = (f32[2,8,256,128]{3,2,1,0:T(8,128)S(1)}, f32[2,8,256,128]{3,2,1,0:T(8,128)}, u32[]{:S(2)}) copy-start(f32[2,8,256,128]{3,2,1,0:T(8,128)} %get-tuple-element.237) | copy-start | bytes 6291460 | tf_op jit(solution)/shard_map/while/body/eval_jaxpr/cond
  54.8 1.4 %copy-start.1 = (f32[2,8,256,128]{3,2,1,0:T(8,128)}, f32[2,8,256,128]{3,2,1,0:T(8,128)S(1)}, u32[]{:S(2)}) copy-start(f32[2,8,256,128]{3,2,1,0:T(8,128)S(1)} %multiply_add_fusion) | copy-start | bytes 6291460 | tf_op jit(solution)/shard_map/while/body/eval_jaxpr/cond
  63.7 3.5 %copy-start = (f32[2,8,256,128]{3,2,1,0:T(8,128)S(1)}, f32[2,8,256,128]{3,2,1,0:T(8,128)}, u32[]{:S(2)}) copy-start(f32[2,8,256,128]{3,2,1,0:T(8,128)} %get-tuple-element.237) | copy-start | bytes 6291460 | tf_op jit(solution)/shard_map/while/body/eval_jaxpr/cond
  70.6 1.4 %copy-start.1 = (f32[2,8,256,128]{3,2,1,0:T(8,128)}, f32[2,8,256,128]{3,2,1,0:T(8,128)S(1)}, u32[]{:S(2)}) copy-start(f32[2,8,256,128]{3,2,1,0:T(8,128)S(1)} %multiply_add_fusion) | copy-start | bytes 6291460 | tf_op jit(solution)/shard_map/while/body/eval_jaxpr/cond
where the time goes:
time: 77.3 us; the launch traced here: 76.9 us
  blocking collectives  32.7 us (42%)
  local copies, waits for them, and re-layouts  17.1 us (22%)
  other arithmetic  13.6 us (18%)
  matrix products  9.64 us (12%)
  between operations  2.06 us (3%)
  loops' own time  1.84 us (2%)
    all_gather x1, blocking collectives, local(): value_piece = lax.all_gather(values, 'seq', axis=0, tiled=True)  16.4 us
    all_gather x1, blocking collectives, local(): key_piece = lax.all_gather(keys, 'seq', axis=0, tiled=True)  16.3 us
    dot_general x2, matrix products, attend_block(): jnp.einsum('kgrp,pkd->kgrd', weights.astype(jnp.bfloat16), values_split,...  6.81 us
    unnamed x5, local copies, waits for them, and re-layouts  5.16 us
    reduce_sum x2, other arithmetic, attend_block(): denominator = query_state[1] * factor + jnp.sum(weights, axis=-1)  4.01 us
    dynamic_slice x4, local copies, waits for them, and re-layouts, local(): lax.scan(one_block, (states, page_store), (key_blocks, value_blocks, jnp....  3.47 us
    dot_general x2, matrix products, attend_block(): jnp.einsum('rkgd,pkd->kgrp', query_block, keys_split, preferred_element_t...  2.83 us
    cond x10, local copies, waits for them, and re-layouts  2.71 us

commit v1 on v0

--- a/solution.py
+++ b/solution.py
@@ -7,6 +7,16 @@
 HEAD_SIZE = 128
 PAGE_TOKENS = 128
 NEG_FILL = -1e30
+
+
+def attach_the_region(in_array, row_data, axis_tag="seq"):
+    return jnp.split(
+        lax.all_gather(
+            jnp.concatenate([in_array, row_data], 1), tiled=True, axis_name=axis_tag, axis=0
+        ),
+        [in_array.shape[1]],
+        1,
+    )
 
 
 def blank_state(kv_heads, group_size, query_count):
@@ -115,8 +125,7 @@
         (blank_state(kv_heads, group_size, part_rows.shape[0]) for part_rows in query_parts)
     )
     page_store = jnp.zeros((slots, PAGE_TOKENS, 2 * kv_width), jnp.bfloat16)
-    key_piece = lax.all_gather(keys, "seq", axis=0, tiled=True)
-    value_piece = lax.all_gather(values, "seq", axis=0, tiled=True)
+    key_piece, value_piece = attach_the_region(keys, values)
     block_count = key_piece.shape[0] // shard_rows
     per_step = max(1, min(block_count, 512 // shard_rows))
     while block_count % per_step:

time: 77.3 us -> 85.9 us (1.11); the launches traced: 76.9 us -> 84.5 us
  blocking collectives: 32.7 us -> 0 us
  waiting for transfers between devices: 0 us -> 23.3 us
  between operations: 2.06 us -> 15.4 us
  local copies, waits for them, and re-layouts: 17.1 us -> 19.2 us
  other arithmetic: 13.6 us -> 15.3 us
    all_gather x2 -> x0, blocking collectives: 32.7 us -> none  [the longest x1 16.4 us: local(): value_piece = lax.all_gather(values, 'seq', axis=0, tiled=True)]
    all_gather x0 -> x1, waiting for transfers between devices: none -> 23.3 us  [attach_the_region(): lax.all_gather(jnp.concatenate([in_array, row_data], 1), tiled=True, axis...]
    split x0 -> x1, local copies, waits for them, and re-layouts: none -> 2.23 us  [attach_the_region(): jnp.split(lax.all_gather(jnp.concatenate([in_array, row_data], 1), tiled=...]
    concatenate x0 -> x1, other arithmetic: none -> 1.69 us  [attach_the_region(): jnp.concatenate([in_array, row_data], 1)]
  transfers between devices with their start and end apart: 0 -> 1, of which waited for: 0 -> 1; matrix products, arithmetic and copies ran while one was open for 0% -> 5% of each run, Pallas kernels for 0% -> 0%
where the time goes in v1:
time: 85.9 us; the launch traced here: 84.5 us
  waiting for transfers between devices  23.3 us (27%)
  local copies, waits for them, and re-layouts  19.2 us (22%)
  between operations  15.4 us (18%)
  other arithmetic  15.3 us (18%)
  matrix products  9.64 us (11%)
  loops' own time  1.7 us (2%)
    all_gather x1, waiting for transfers between devices, attach_the_region(): lax.all_gather(jnp.concatenate([in_array, row_data], 1), tiled=True, axis...  23.3 us
    dot_general x2, matrix products, attend_block(): jnp.einsum('kgrp,pkd->kgrd', weights.astype(jnp.bfloat16), values_split,...  6.8 us
    unnamed x5, local copies, waits for them, and re-layouts  5.15 us
    reduce_sum x2, other arithmetic, attend_block(): denominator = query_state[1] * factor + jnp.sum(weights, axis=-1)  4.01 us
    dynamic_slice x4, local copies, waits for them, and re-layouts, local(): lax.scan(one_block, (states, page_store), (key_blocks, value_blocks, jnp....  3.41 us
    dot_general x2, matrix products, attend_block(): jnp.einsum('rkgd,pkd->kgrp', query_block, keys_split, preferred_element_t...  2.83 us
    cond x10, local copies, waits for them, and re-layouts  2.71 us
    split x1, local copies, waits for them, and re-layouts, attach_the_region(): jnp.split(lax.all_gather(jnp.concatenate([in_array, row_data], 1), tiled=...  2.23 us
  transfers between devices with their start and end apart: 1, of which 1 were waited for; matrix products, arithmetic and copies ran while one was open for 5% of the time, Pallas kernels for 0%

profile of v1, /device:TPU:26, one launch (start us, length us, event | category | flops | bytes accessed | tf_op | source)
XLA Modules:
  0.0 84.5 jit_solution(5130663248949104899)
XLA Ops:
  7.2 1.7 %pad_maximum_fusion.1 = bf16[256,512]{1,0:T(8,128)(2,1)} fusion(bf16[256,256]{1,0:T(8,128)(2,1)} %param.11, bf16[256,256]{1,0:T(8,128)(2,1)} %param.10), kind=kLoop, calls=%fused_computation.36 | loop fusion | flops 524288 | bytes 524288 | tf_op jit(solution)/shard_map/concatenate | solution.py:15
  9.6 0.6 slice.5
  10.2 0.8 copy.34
  10.9 0.1 broadcast_in_dim_reshape.2
  11.0 1.5 %copy.33 = bf16[256,2048]{0,1:T(8,128)(2,1)S(1)} copy(bf16[256,2048]{1,0:T(8,128)(2,1)} %param.9) | data formatting | bytes 2097152 | tf_op args[0]
  12.5 0.7 copy.35
  13.9 0.2 convert_reduce_fusion
  14.0 0.1 fusion.20
  14.2 0.1 select_reduce_fusion
  14.3 23.3 %all-gather.2.cloned.1.call-done = bf16[1024,512]{1,0:T(8,128)(2,1)} async-done(((bf16[256,512]{1,0:T(8,128)(2,1)}), bf16[1024,512]{1,0:T(8,128)(2,1)}) %all-gather.2.cloned.1.call-update) | async-done | bytes 1048592 | tf_op jit(solution)/shard_map/all_gather | solution.py:14
  37.5 2.2 %fusion.21 = (bf16[1024,256]{1,0:T(8,128)(2,1)}, bf16[1024,256]{1,0:T(8,128)(2,1)}) fusion(bf16[1024,512]{1,0:T(8,128)(2,1)} %all-gather.2.cloned.1.call-done), kind=kLoop, calls=%fused_computation.48 | loop fusion | bytes 2097152 | tf_op jit(solution)/shard_map/split | solution.py:13
  39.8 1.6 %broadcast_in_dim.106 = f32[2,8,256,128]{3,2,1,0:T(8,128)} broadcast(f32[]{:T(128)} %constant.102.clone.1), dimensions={} | broadcast | bytes 2097156 | tf_op jit(solution)/shard_map/broadcast_in_dim | solution.py:26
  41.4 31.3 %while.20 = (s32[]{:T(128)}, f32[2,8,256]{2,1,0:T(8,128)S(1)}, f32[2,8,256]{2,1,0:T(8,128)S(1)}, f32[2,8,256,128]{3,2,1,0:T(8,128)}, bf16[4,128,512]{1,2,0:T(8,1...) while((s32[]{:T(128)}, f32[2,8,256]{2,1,0:T(8,128)S(1)}, ...), condition=%wide.region_8.9_spmd.clone, body=%wide.region_3.8_spmd.clone.sunk | while | flops 1103377152 | bytes 57424572 | solution.py:166
  41.4 0.6 dynamic_slice.31
  42.7 0.7 add_compare_fusion.2
  43.4 1.1 %constant_dynamic-slice_fusion.3 = (bf16[1,512,256]{2,1,0:T(8,128)(2,1)S(1)}, bf16[1,512,256]{2,1,0:T(8,128)(2,1)S(1)}) fusion(bf16[2,512,256]{2,1,0:T(8,128)(2,1)} %get-tuple-element.558, s32[]{:T(128)S(6)} %copy.67, bf16[2,512,256]{2,1,0:T(8,128)(2,1)} %get-tuple-element.557), kind=kLoop, calls=%fused_computation.31.clone.1 | loop fusion | bytes 1048580 | tf_op jit(solution)/shard_map/while/body/jit(dynamic_index_in_dim)/dynamic_slice | solution.py:166
  44.6 1.1 %broadcast_select_fusion.4 = (bf16[4,128,2,1,128]{4,2,1,0,3:T(2,128)(2,1)S(1)}, bf16[4,128,2,1,128]{4,2,1,0,3:T(2,128)(2,1)S(1)}) fusion(bf16[4,128,2,1,128]{4,2,1,0,3:T(2,128)(2,1)S(1)} %squeeze.31, pred[4,128]{1,0:T(4,128)(4,1)S(1)} %add_compare_fusion.2, bf16[4,128,2,1,128]{4,2,1,0,3:T(2,128)(2,1)S(1)} %squeeze.32), kind=kLoop, calls=%fused_computation.25.clone.1 | loop fusion | flops 262144 | bytes 1049088 | tf_op jit(solution)/shard_map/while/body/eval_jaxpr/jit(_where)/select_n | solution.py:96
  45.7 0.7 pad_maximum_fusion.3
  46.4 0.4 copy.55
  46.9 0.6 gather_fusion
  47.6 0.2 select_select_fusion.2
  47.7 9.3 %conditional.3 = ((f32[2,8,256]{2,1,0:T(8,128)S(1)}, f32[2,8,256]{2,1,0:T(8,128)S(1)}, f32[2,8,256,128]{3,2,1,0:T(8,128)})) conditional(s32[]{:T(128)} %convert_element_type.41, (f32[2,8,256]{2,1,0:T(8,128)S(1)}, f32[2,8,256]{2,1,0:T(8,128)S(1)}, f32[2,8,256,128]{3,2,1,0:T(8,128)}) %tuple.63, (s32[]{:T(128)}, s32[]{:T(128)}, s32[]{:T(128)}, ...), branch_computations={%region_4.4_spmd, %region_5.7_spmd} | conditional | flops 1102325504 | bytes 49553512 | solution.py:146
  47.7 0.7 broadcast_compare_fusion
  48.4 0.2 compare_and_fusion
  48.8 1.4 %fusion.2 = (f32[2,8,256]{2,1,0:T(8,128)S(1)}, f32[2,512,256,8]{2,1,3,0:T(8,128)S(1)}) fusion(pred[256,512]{0,1:T(8,128)(4,1)S(1)} %compare_and_fusion, bf16[256,2,8,128]{3,0,2,1:T(8,128)(2,1)S(1)} %get-tuple-element.235, bf16[512,2,128,1]{2,1,0,3:T(2,128)(2,1)S(1)} %bitcast.45), kind=kOutput, calls=%fused_computation.4 | convolution fusion | flops 543158272 | bytes 9846784 | tf_op jit(solution)/shard_map/while/body/eval_jaxpr/cond/branch_1_fun/rkgd,pkd->kgrp/dot_general | solution.py:37
  50.2 2.0 %fusion.4 = f32[2,8,256]{2,1,0:T(8,128)S(1)} fusion(f32[2,512,256,8]{2,1,3,0:T(8,128)S(1)} %get-tuple-element.398, f32[2,8,256]{2,1,0:T(8,128)S(1)} %max.6, pred[256,512]{0,1:T(8,128)(4,1)S(1)} %compare_and_fusion), kind=kLoop, calls=%fused_computation.6 | loop fusion | flops 10481664 | bytes 8552448 | tf_op jit(solution)/shard_map/while/body/eval_jaxpr/cond/branch_1_fun/reduce_sum | solution.py:48
  52.3 3.4 %multiply_add_fusion = f32[2,8,256,128]{3,2,1,0:T(8,128)S(1)} fusion(f32[2,8,256,128]{3,2,1,0:T(8,128)S(1)} %copy-done, f32[2,512,256,8]{2,1,3,0:T(8,128)S(1)} %get-tuple-element.398, f32[2,8,256]{2,1,0:T(8,128)S(1)} %max.6, pred[256,512]{0,1:T(8,128)(4,1)S(1)} %compare_and_fusion, f32[2,8,256]{2,1,0:T(8,128)S(1)} %get-tuple-element.396, ...), kind=kOutput, calls=%fused_computation.9 | convolution fusion | flops 548405248 | bytes 13008896 | tf_op jit(solution)/shard_map/while/body/eval_jaxpr/cond/branch_1_fun/kgrp,pkd->kgrd/dot_general | solution.py:49
  55.7 1.3 %copy-done.1 = f32[2,8,256,128]{3,2,1,0:T(8,128)} copy-done((f32[2,8,256,128]{3,2,1,0:T(8,128)}, f32[2,8,256,128]{3,2,1,0:T(8,128)S(1)}, u32[]{:S(2)}) %copy-start.1) | copy-done | bytes 2097176 | tf_op jit(solution)/shard_map/while/body/eval_jaxpr/cond
  57.0 0.6 dynamic_slice.31
  58.3 0.7 add_compare_fusion.2
  59.0 1.1 %constant_dynamic-slice_fusion.3 = (bf16[1,512,256]{2,1,0:T(8,128)(2,1)S(1)}, bf16[1,512,256]{2,1,0:T(8,128)(2,1)S(1)}) fusion(bf16[2,512,256]{2,1,0:T(8,128)(2,1)} %get-tuple-element.558, s32[]{:T(128)S(6)} %copy.67, bf16[2,512,256]{2,1,0:T(8,128)(2,1)} %get-tuple-element.557), kind=kLoop, calls=%fused_computation.31.clone.1 | loop fusion | bytes 1048580 | tf_op jit(solution)/shard_map/while/body/jit(dynamic_index_in_dim)/dynamic_slice | solution.py:166
  60.2 1.1 %broadcast_select_fusion.4 = (bf16[4,128,2,1,128]{4,2,1,0,3:T(2,128)(2,1)S(1)}, bf16[4,128,2,1,128]{4,2,1,0,3:T(2,128)(2,1)S(1)}) fusion(bf16[4,128,2,1,128]{4,2,1,0,3:T(2,128)(2,1)S(1)} %squeeze.31, pred[4,128]{1,0:T(4,128)(4,1)S(1)} %add_compare_fusion.2, bf16[4,128,2,1,128]{4,2,1,0,3:T(2,128)(2,1)S(1)} %squeeze.32), kind=kLoop, calls=%fused_computation.25.clone.1 | loop fusion | flops 262144 | bytes 1049088 | tf_op jit(solution)/shard_map/while/body/eval_jaxpr/jit(_where)/select_n | solution.py:96
  61.4 0.7 pad_maximum_fusion.3
  62.1 0.4 copy.55
  62.6 0.6 gather_fusion
  63.2 0.2 select_select_fusion.2
  63.4 9.3 %conditional.3 = ((f32[2,8,256]{2,1,0:T(8,128)S(1)}, f32[2,8,256]{2,1,0:T(8,128)S(1)}, f32[2,8,256,128]{3,2,1,0:T(8,128)})) conditional(s32[]{:T(128)} %convert_element_type.41, (f32[2,8,256]{2,1,0:T(8,128)S(1)}, f32[2,8,256]{2,1,0:T(8,128)S(1)}, f32[2,8,256,128]{3,2,1,0:T(8,128)}) %tuple.63, (s32[]{:T(128)}, s32[]{:T(128)}, s32[]{:T(128)}, ...), branch_computations={%region_4.4_spmd, %region_5.7_spmd} | conditional | flops 1102325504 | bytes 49553512 | solution.py:146
  63.4 0.7 broadcast_compare_fusion
  64.1 0.2 compare_and_fusion
  64.4 0.1 reshape.145
  64.4 1.4 %fusion.2 = (f32[2,8,256]{2,1,0:T(8,128)S(1)}, f32[2,512,256,8]{2,1,3,0:T(8,128)S(1)}) fusion(pred[256,512]{0,1:T(8,128)(4,1)S(1)} %compare_and_fusion, bf16[256,2,8,128]{3,0,2,1:T(8,128)(2,1)S(1)} %get-tuple-element.235, bf16[512,2,128,1]{2,1,0,3:T(2,128)(2,1)S(1)} %bitcast.45), kind=kOutput, calls=%fused_computation.4 | convolution fusion | flops 543158272 | bytes 9846784 | tf_op jit(solution)/shard_map/while/body/eval_jaxpr/cond/branch_1_fun/rkgd,pkd->kgrp/dot_general | solution.py:37
  65.9 2.0 %fusion.4 = f32[2,8,256]{2,1,0:T(8,128)S(1)} fusion(f32[2,512,256,8]{2,1,3,0:T(8,128)S(1)} %get-tuple-element.398, f32[2,8,256]{2,1,0:T(8,128)S(1)} %max.6, pred[256,512]{0,1:T(8,128)(4,1)S(1)} %compare_and_fusion), kind=kLoop, calls=%fused_computation.6 | loop fusion | flops 10481664 | bytes 8552448 | tf_op jit(solution)/shard_map/while/body/eval_jaxpr/cond/branch_1_fun/reduce_sum | solution.py:48
  67.9 3.4 %multiply_add_fusion = f32[2,8,256,128]{3,2,1,0:T(8,128)S(1)} fusion(f32[2,8,256,128]{3,2,1,0:T(8,128)S(1)} %copy-done, f32[2,512,256,8]{2,1,3,0:T(8,128)S(1)} %get-tuple-element.398, f32[2,8,256]{2,1,0:T(8,128)S(1)} %max.6, pred[256,512]{0,1:T(8,128)(4,1)S(1)} %compare_and_fusion, f32[2,8,256]{2,1,0:T(8,128)S(1)} %get-tuple-element.396, ...), kind=kOutput, calls=%fused_computation.9 | convolution fusion | flops 548405248 | bytes 13008896 | tf_op jit(solution)/shard_map/while/body/eval_jaxpr/cond/branch_1_fun/kgrp,pkd->kgrd/dot_general | solution.py:49
  71.3 1.3 %copy-done.1 = f32[2,8,256,128]{3,2,1,0:T(8,128)} copy-done((f32[2,8,256,128]{3,2,1,0:T(8,128)}, f32[2,8,256,128]{3,2,1,0:T(8,128)S(1)}, u32[]{:S(2)}) %copy-start.1) | copy-done | bytes 2097176 | tf_op jit(solution)/shard_map/while/body/eval_jaxpr/cond
  72.7 2.0 %fusion.17 = bf16[256,2,8,128]{3,0,2,1:T(8,128)(2,1)S(1)} fusion(f32[2,8,256,128]{3,2,1,0:T(8,128)} %get-tuple-element.262, f32[2,8,256]{2,1,0:T(8,128)S(1)} %broadcast_select_fusion.2, pred[256]{0:T(512)(128)(4,1)S(1)} %broadcast_compare_fusion.1), kind=kLoop, calls=%fused_computation.35 | loop fusion | flops 1572864 | bytes 3162368 | tf_op jit(solution)/shard_map/convert_element_type | solution.py:63
  74.7 0.7 copy.36
  75.4 1.2 %copy.53 = bf16[32,8,16,128]{3,1,2,0:T(8,128)(2,1)} copy(bf16[32,8,16,128]{3,2,1,0:T(8,128)(2,1)S(1)} %bitcast.47) | data formatting | bytes 2097152
  76.6 1.0 %copy.37 = bf16[4,128,512]{2,1,0:T(8,128)(2,1)} copy(bf16[4,128,512]{1,2,0:T(8,128)(2,1)S(1)} %get-tuple-element.363) | data formatting | bytes 1048576
  (41 shorter events, 0.7 us)
Async XLA Ops:
  7.2 30.4 %all-gather.2.cloned.1.call-start = ((), (), s32[]{:S(2)}) async-start(), calls=%async_computation | async-start | bytes 1310720 | tf_op jit(solution)/shard_map/all_gather | solution.py:14
  48.8 3.5 %copy-start = (f32[2,8,256,128]{3,2,1,0:T(8,128)S(1)}, f32[2,8,256,128]{3,2,1,0:T(8,128)}, u32[]{:S(2)}) copy-start(f32[2,8,256,128]{3,2,1,0:T(8,128)} %get-tuple-element.237) | copy-start | bytes 6291460 | tf_op jit(solution)/shard_map/while/body/eval_jaxpr/cond
  55.7 1.4 %copy-start.1 = (f32[2,8,256,128]{3,2,1,0:T(8,128)}, f32[2,8,256,128]{3,2,1,0:T(8,128)S(1)}, u32[]{:S(2)}) copy-start(f32[2,8,256,128]{3,2,1,0:T(8,128)S(1)} %multiply_add_fusion) | copy-start | bytes 6291460 | tf_op jit(solution)/shard_map/while/body/eval_jaxpr/cond
  64.4 3.5 %copy-start = (f32[2,8,256,128]{3,2,1,0:T(8,128)S(1)}, f32[2,8,256,128]{3,2,1,0:T(8,128)}, u32[]{:S(2)}) copy-start(f32[2,8,256,128]{3,2,1,0:T(8,128)} %get-tuple-element.237) | copy-start | bytes 6291460 | tf_op jit(solution)/shard_map/while/body/eval_jaxpr/cond
  71.3 1.4 %copy-start.1 = (f32[2,8,256,128]{3,2,1,0:T(8,128)}, f32[2,8,256,128]{3,2,1,0:T(8,128)S(1)}, u32[]{:S(2)}) copy-start(f32[2,8,256,128]{3,2,1,0:T(8,128)S(1)} %multiply_add_fusion) | copy-start | bytes 6291460 | tf_op jit(solution)/shard_map/while/body/eval_jaxpr/cond
Sparse Core Ops, SparseCore 0:
  10.1 27.3 all-gather.1
